TPU v7x, 256 devices: a whole 4x4x8 slice. The times are simulated.
256 devices in a mesh: gx: 16 (over y, z_hi, core), gy: 4 (over z_lo), gz: 4 (over x).
Axes of the slice: x: 4, y: 4, z: 8 (z_hi: 2, z_lo: 4; z = z_hi * 4 + z_lo), core: 2. Of those that a mesh axis runs over, the one named last changes fastest.
Arguments:
- atom_cell: int32 [3, 65536], P(None, ('gx', 'gy', 'gz')), may hold values from 0 to 63, as said below
- atom_frac: bfloat16 [3, 65536], P(None, ('gx', 'gy', 'gz')), may hold values from 0 to 1
- features: bfloat16 [128, 65536], P(None, ('gx', 'gy', 'gz')), may hold values from -6 to 6
- ghost_export: int32 [16384], P(('gx', 'gy', 'gz')), may hold values from 0 to 255, as said below
- neighbors: int32 [65536, 32], P(('gx', 'gy', 'gz')), may hold values from 0 to 1983, as said below
- neighbor_count: int32 [65536], P(('gx', 'gy', 'gz')), may hold values from 16 to 32
- w_up: bfloat16 [128, 128], replicated, may hold values from -0.5 to 0.5
- radial_weight: float32 [128, 8], replicated, may hold values from -2 to 2
- w_out: bfloat16 [128, 128], replicated, may hold values from -0.5 to 0.5
- energy_weight: bfloat16 [128], replicated, may hold values from -0.5 to 0.5
- charge_weight: bfloat16 [128], replicated, may hold values from -0.5 to 0.5
Outputs:
- forces: float32 [3, 65536], P(None, ('gx', 'gy', 'gz'))
- atom_energy: float32 [65536], P(('gx', 'gy', 'gz'))
Inputs may be any that keep to these rules, and one draw needn't show every extreme that they name: `atom_cell`: every atom whose cell is the first or one of the last two along some dimension of its domain is in its domain's ghost_export list. `ghost_export`: 64 distinct local atom indices of each domain. `neighbors`: each row names distinct entries of its domain's table, never the atom itself and never slot 13. Only the first neighbor_count entries of a row are neighbours.
All inputs are finite; a program needn't handle non-finite values.
Results may differ from a plain program's by a relative error of at most 0.0025.
Values may be sent and summed in bfloat16 or wider, within the bound.
A program may use at most 64 MiB of HBM per device.

v0:
```python
import math

import jax
import jax.numpy as jnp
import numpy as np
from jax import lax
from jax.experimental import pallas as pl
from jax.experimental.pallas import tpu as pltpu
from jax.sharding import PartitionSpec as P

CX, CY, CZ = 8, 16, 64
HALO_X, HALO_Y, HALO_Z = CX + 3, CY + 3, CZ + 3
PER_HALF = 128 // HALO_Y
NX, NY, NZ = 16, 4, 4
PLANES = NX * NY
NEIGHBORS = 32
EXPORTED = 64
ATOMS = 256
CHANNELS = 128
ROWS = CHANNELS + 16
BLOCKS = 8

basis_step = 1.4
basis_width = 1.4
message_scale = 0.125
vector_scale = 1.0 / 6.0
ewald_beta_sq = 2.0

F32 = jnp.float32
BF16 = jnp.bfloat16
MESH = pl.DeviceIdType.MESH
HIGHEST = lax.Precision.HIGHEST

SLOTS = [(s, s // 9 - 1, s // 3 % 3 - 1, s % 3 - 1) for s in range(27)]
LENT = [slot for slot in SLOTS if slot[0] != 13]
WINDOWS = [(x, x // PER_HALF, HALO_Y * (x % PER_HALF)) for x in range(HALO_X)]


def trig_basis(extent):
    cells = np.arange(extent)
    half = extent // 2
    rows, numbers = [], []
    for k in range(half + 1):
        scale = math.sqrt((1.0 if k in (0, half) else 2.0) / extent)
        rows.append(scale * np.cos(2.0 * math.pi * (k * cells % extent) / extent))
        numbers.append(k)
    for k in range(1, half):
        rows.append(math.sqrt(2.0 / extent) * np.sin(2.0 * math.pi * (k * cells % extent) / extent))
        numbers.append(k)
    return np.array(rows), np.array(numbers)


def tables():
    wave_x, number_x = trig_basis(CX * NX)
    wave_y, number_y = trig_basis(CY * NY)
    wave_z, _ = trig_basis(CZ * NZ)
    along_z = np.zeros((NZ, CZ * NZ, 128), np.float32)
    for l in range(NZ):
        along_z[l, :, :HALO_Z] = wave_z[:, (l * CZ - 1 + np.arange(HALO_Z)) % (CZ * NZ)]
    along_x = np.zeros((CX * NX, 256), np.float32)
    for x in range(HALO_X):
        for i in range(NX):
            along_x[:, x * NX + i] = wave_x[:, (i * CX + x - 1) % (CX * NX)]
    along_y = np.zeros((128, 128), np.float32)
    for j in range(NY):
        for y in range(HALO_Y):
            along_y[: CY * NY, 32 * j + y] = wave_y[:, (j * CY + y - 1) % (CY * NY)]
    square = np.zeros((128, 128), np.float32)
    square[:, : CY * NY] = (2.0 * math.pi / (CX * NX) * number_x[:, None]) ** 2 + (
        2.0 * math.pi / (CY * NY) * number_y[None, :]
    ) ** 2
    square[:, CY * NY :] = 1.0
    return along_z, along_x, along_x.T.copy(), along_y, along_y.T.copy(), square


def spline_weights(t):
    r = 1.0 - t
    t2 = t * t
    t3 = t2 * t
    values = (
        r * r * r / 6.0,
        (3.0 * t3 - 6.0 * t2 + 4.0) / 6.0,
        (-3.0 * t3 + 3.0 * t2 + 3.0 * t + 1.0) / 6.0,
        t3 / 6.0,
    )
    slopes = (-0.5 * r * r, 1.5 * t2 - 2.0 * t, -1.5 * t2 + t + 0.5, 0.5 * t2)
    return values, slopes


def node_rows(count, cell, parts):
    gap = lax.broadcasted_iota(jnp.int32, (count, ATOMS), 0) - cell
    total = jnp.zeros((count, ATOMS), F32)
    for s in range(4):
        total = jnp.where(gap == s, parts[s], total)
    return total


def dot(a, b, precision=None):
    return jnp.dot(a, b, precision=precision, preferred_element_type=F32)


def dot_nt(a, b, precision=None):
    return lax.dot_general(
        a, b, (((1,), (1,)), ((), ())), precision=precision, preferred_element_type=F32
    )


def halves(x):
    high = x.astype(BF16).astype(F32)
    return high, x - high


def kernel(
    cell_ref,
    frac_ref,
    feat_ref,
    export_ref,
    neighbor_ref,
    count_ref,
    w_up_ref,
    radial_ref,
    w_out_ref,
    energy_ref,
    charge_ref,
    along_z_ref,
    along_x_ref,
    along_xt_ref,
    along_y_ref,
    along_yt_ref,
    square_ref,
    forces_ref,
    atom_energy_ref,
    parts_out,
    parts_in,
    planes_out,
    planes_in,
    back_out,
    back_in,
    modes,
    lend_out,
    ghosts,
    grads_out,
    grads_in,
    place,
    z_waves,
    z_slopes,
    window,
    table,
    gathered,
    radials,
    messages,
    turned,
    hots,
    lows,
    highs,
    relatives,
    inverses,
    sums,
    pushed,
    parts_send,
    parts_recv,
    planes_send,
    planes_recv,
    back_send,
    back_recv,
    modes_send,
    modes_recv,
    lend_send,
    lend_recv,
    grads_send,
    grads_recv,
):
    gx, gy, gz = lax.axis_index("gx"), lax.axis_index("gy"), lax.axis_index("gz")
    me = gy * NX + gx

    def shifted(a, b, c):
        return (lax.rem(gx + a + NX, NX), lax.rem(gy + b + NY, NY), lax.rem(gz + c + NZ, NZ))

    def over_planes(action):
        for dy in range(NY):

            def step(dx, carry):
                x, y = lax.rem(gx + dx, NX), lax.rem(gy + dy, NY)
                action(x, y, y * NX + x)
                return carry

            lax.fori_loop(1 if dy == 0 else 0, NX, step, 0)

    barrier = pltpu.get_barrier_semaphore()

    def greet(device):
        pl.semaphore_signal(barrier, inc=1, device_id=device, device_id_type=MESH)

    for c in range(1, NZ):
        greet((gx, gy, lax.rem(gz + c, NZ)))
    over_planes(lambda x, y, p: greet((x, y, gz)))
    for s, a, b, c in LENT:
        greet(shifted(-a, -b, -c))

    feat = feat_ref[...]
    cell = cell_ref[...]
    frac = frac_ref[...].astype(F32)
    up = dot(w_up_ref[...], feat).astype(BF16)
    charge = dot(jnp.broadcast_to(charge_ref[...], (16, CHANNELS)), feat)[0:1, :]
    place[...] = jnp.zeros_like(place)
    place[0:3, :] = cell.astype(F32)
    place[8:11, :] = frac
    spot = place[...]
    export = export_ref[...]
    pick_t = (lax.broadcasted_iota(jnp.int32, (ATOMS, 128), 0) == export).astype(F32)
    pick = pick_t.T
    lend_out[0:EXPORTED, :] = dot_nt(pick[0:EXPORTED].astype(BF16), up).astype(BF16)
    lend_out[EXPORTED : EXPORTED + 16, :] = dot(spot.astype(BF16), pick_t.astype(BF16)).astype(BF16)

    values, slopes = spline_weights(frac)
    along_z = along_z_ref[gz]
    z_waves[...] = dot(
        along_z, node_rows(128, cell[2:3], [v[2:3] for v in values]), HIGHEST
    )
    rows_x = node_rows(16, cell[0:1], [v[0:1] for v in values])
    rows_y = node_rows(24, cell[1:2], [v[1:2] for v in values])
    window[...] = jnp.zeros_like(window)
    for x, half, lane in WINDOWS:
        at = pl.ds(128 * half + lane, HALO_Y)
        window[at, 0:ATOMS] = rows_x[x : x + 1] * rows_y[0:HALO_Y]
    waves = dot_nt(z_waves[...] * charge, window[:, 0:ATOMS], HIGHEST)
    for l in range(NZ):
        parts_out[l] = waves[PLANES * l : PLANES * (l + 1)]

    pl.semaphore_wait(barrier, (NZ - 1) + (PLANES - 1) + len(LENT))

    def part_copy(c):
        l = lax.rem(gz + c, NZ)
        return pltpu.make_async_remote_copy(
            src_ref=parts_out.at[l],
            dst_ref=parts_in.at[gz],
            send_sem=parts_send.at[c],
            recv_sem=parts_recv.at[NZ - c],
            device_id=(gx, gy, l),
            device_id_type=MESH,
        )

    def part_arrival(c):
        l = lax.rem(gz + c, NZ)
        return pltpu.make_async_remote_copy(
            src_ref=parts_out.at[l],
            dst_ref=parts_in.at[l],
            send_sem=parts_send.at[c],
            recv_sem=parts_recv.at[c],
            device_id=(gx, gy, l),
            device_id_type=MESH,
        )

    def lend_copy(s, a, b, c):
        return pltpu.make_async_remote_copy(
            src_ref=lend_out,
            dst_ref=ghosts.at[s],
            send_sem=lend_send.at[s],
            recv_sem=lend_recv.at[s],
            device_id=shifted(-a, -b, -c),
            device_id_type=MESH,
        )

    for c in range(1, NZ):
        part_copy(c).start()
    for slot in LENT:
        lend_copy(*slot).start()

    z_slopes[...] = dot(
        along_z, node_rows(128, cell[2:3], [v[2:3] for v in slopes]), HIGHEST
    )
    slope_x = node_rows(16, cell[0:1], [v[0:1] for v in slopes])
    slope_y = node_rows(24, cell[1:2], [v[1:2] for v in slopes])
    for x, half, lane in WINDOWS:
        at = pl.ds(128 * half + lane, HALO_Y)
        window[at, ATOMS : 2 * ATOMS] = slope_x[x : x + 1] * rows_y[0:HALO_Y]
        window[at, 2 * ATOMS : 3 * ATOMS] = rows_x[x : x + 1] * slope_y[0:HALO_Y]
    parts_in[gz] = parts_out[gz]
    ghosts[13] = jnp.zeros((EXPORTED + 16, 128), BF16)
    ghosts[27] = jnp.zeros((EXPORTED + 16, 128), BF16)
    table[0:CHANNELS, :] = up
    table[CHANNELS:ROWS, :] = spot.astype(BF16)

    for c in range(1, NZ):
        part_arrival(c).wait_recv()
    total = parts_in[0] + parts_in[1] + parts_in[2] + parts_in[3]
    planes_out[:, 0, :] = total[:, 0:128]
    planes_out[:, 1, :] = total[:, 128:256]

    def plane_copy(x, y, p):
        return pltpu.make_async_remote_copy(
            src_ref=planes_out.at[p],
            dst_ref=planes_in.at[me],
            send_sem=planes_send,
            recv_sem=planes_recv,
            device_id=(x, y, gz),
            device_id_type=MESH,
        )

    over_planes(lambda x, y, p: plane_copy(x, y, p).start())
    planes_in[me] = planes_out[me]

    for slot in LENT:
        lend_copy(*slot).wait_recv()
    row = lax.broadcasted_iota(jnp.int32, (16, 128), 0)
    lane = lax.broadcasted_iota(jnp.int32, (16, 128), 1)
    for h in range(1, BLOCKS):
        first = 4 * (h - 1)
        lent = jnp.concatenate([ghosts[first + q, 0:EXPORTED, :] for q in range(4)], axis=0)
        table[ROWS * h : ROWS * h + CHANNELS, :] = lent.astype(F32).T.astype(BF16)
        spots = []
        for q in range(4):
            s = first + q
            a, b, c = (s // 9 - 1, s // 3 % 3 - 1, s % 3 - 1)
            far = jnp.where(
                row == 0,
                float(a * CX),
                jnp.where(row == 1, float(b * CY), jnp.where(row == 2, float(c * CZ), 0.0)),
            )
            spots.append(ghosts[s, EXPORTED : EXPORTED + 16, :].astype(F32) + far)
        at = slice(ROWS * h + CHANNELS, ROWS * (h + 1))
        table[at, 0:128] = jnp.where(lane < EXPORTED, spots[0], spots[1]).astype(BF16)
        table[at, 128:256] = jnp.where(lane < EXPORTED, spots[2], spots[3]).astype(BF16)

    entry = neighbor_ref[...]
    eye = (
        lax.broadcasted_iota(jnp.int32, (NEIGHBORS, NEIGHBORS), 0)
        == lax.broadcasted_iota(jnp.int32, (NEIGHBORS, NEIGHBORS), 1)
    ).astype(BF16)
    lows[...] = dot_nt(eye, (entry & 255).astype(F32).astype(BF16)).astype(jnp.int32)
    highs[...] = dot_nt(eye, (entry >> 8).astype(F32).astype(BF16)).astype(jnp.int32)

    weight_high, weight_low = halves(radial_ref[...])
    stack = lax.broadcasted_iota(jnp.int32, (8, 24), 1)
    basis_row = lax.broadcasted_iota(jnp.int32, (8, 24), 0)
    hit = lax.rem(stack, 8) == basis_row
    to_high = jnp.logical_and(hit, stack < 16).astype(BF16)
    to_low = jnp.logical_and(hit, stack >= 16).astype(BF16)
    weights = (
        dot(weight_high.astype(BF16), to_high) + dot(weight_low.astype(BF16), to_low)
    ).astype(BF16)

    here = spot[0:8] + spot[8:16]
    count = count_ref[...]
    for a in range(4):
        sums[a] = jnp.zeros((CHANNELS, ATOMS), F32)
    sub = lax.broadcasted_iota(jnp.int32, (ATOMS, 2 * ATOMS), 0)
    centre = lax.broadcasted_iota(jnp.int32, (8, 2 * ATOMS), 0).astype(F32) * basis_step

    def gather(pair, carry):
        k = 2 * pair
        low = jnp.concatenate([lows[pl.ds(k, 1), :], lows[pl.ds(k + 1, 1), :]], axis=1)
        high = jnp.concatenate([highs[pl.ds(k, 1), :], highs[pl.ds(k + 1, 1), :]], axis=1)
        hot = jnp.where(sub == low, 1.0, 0.0).astype(BF16)
        hots[pair] = hot
        gathered[...] = dot(table[...], hot)
        high8 = jnp.broadcast_to(high, (8, 2 * ATOMS))

        def chosen(start):
            result = gathered[pl.ds(start, 8), :]
            for h in range(1, BLOCKS):
                result = jnp.where(high8 == h, gathered[pl.ds(start + ROWS * h, 8), :], result)
            return result

        there = chosen(CHANNELS) + chosen(CHANNELS + 8)
        rel = there - jnp.concatenate([here, here], axis=1)
        dist = jnp.sqrt(jnp.sum(rel * rel, axis=0, keepdims=True) + 1.0)
        used = jnp.concatenate([count > k, count > k + 1], axis=1).astype(F32)
        gap = (dist - centre) / basis_width
        basis = jnp.exp(-(gap * gap)) * used
        slope = basis * gap * (-2.0 / basis_width)
        basis_high, basis_low = halves(basis)
        slope_high, slope_low = halves(slope)
        radials[0:CHANNELS, :] = dot(
            weights, jnp.concatenate([basis_high, basis_low, basis_high], axis=0).astype(BF16)
        )
        radials[CHANNELS : 2 * CHANNELS, :] = dot(
            weights, jnp.concatenate([slope_high, slope_low, slope_high], axis=0).astype(BF16)
        )
        inverse = 1.0 / dist
        relatives[k] = rel[:, 0:ATOMS]
        relatives[k + 1] = rel[:, ATOMS:]
        inverses[k] = jnp.broadcast_to(inverse[:, 0:ATOMS], (8, ATOMS))
        inverses[k + 1] = jnp.broadcast_to(inverse[:, ATOMS:], (8, ATOMS))
        along = [jnp.broadcast_to(rel[a : a + 1], (8, 2 * ATOMS)) for a in range(3)]
        for c in range(0, CHANNELS, 8):
            at = pl.ds(c, 8)
            source = chosen(c)
            message = radials[at, :] * source
            turn = radials[pl.ds(CHANNELS + c, 8), :] * source
            messages[k, at, :] = message[:, 0:ATOMS]
            messages[k + 1, at, :] = message[:, ATOMS:]
            turned[k, at, :] = turn[:, 0:ATOMS]
            turned[k + 1, at, :] = turn[:, ATOMS:]
            sums[0, at, :] += message[:, 0:ATOMS] + message[:, ATOMS:]
            for a in range(3):
                moved = message * along[a]
                sums[a + 1, at, :] += moved[:, 0:ATOMS] + moved[:, ATOMS:]
        return carry

    lax.fori_loop(0, NEIGHBORS // 2, gather, 0)

    scalar = sums[0] * message_scale
    vector = [sums[a + 1] * (message_scale * vector_scale) for a in range(3)]
    invariant = scalar + scalar * scalar + (
        vector[0] * vector[0] + vector[1] * vector[1] + vector[2] * vector[2]
    )
    w_out = w_out_ref[...]
    hidden = feat.astype(F32) + dot(w_out, invariant.astype(BF16))
    wide = (
        lax.broadcasted_iota(jnp.int32, (CHANNELS, CHANNELS), 0)
        == lax.broadcasted_iota(jnp.int32, (CHANNELS, CHANNELS), 1)
    ).astype(BF16)
    readout = dot_nt(wide, jnp.broadcast_to(energy_ref[...], (16, CHANNELS)))[:, 0:1]
    gate = 1.0 / (1.0 + jnp.exp(-hidden))
    short = jnp.sum(readout * (hidden * gate), axis=0, keepdims=True)
    d_hidden = readout * (gate * (1.0 + hidden * (1.0 - gate)))
    back_high, back_low = halves(d_hidden)
    w_out_t = w_out.astype(F32).T.astype(BF16)
    d_invariant = dot(w_out_t, back_high.astype(BF16)) + dot(w_out_t, back_low.astype(BF16))
    d_invariant = d_invariant.astype(BF16).astype(F32)
    sums[0] = d_invariant * (1.0 + 2.0 * scalar) * message_scale
    for a in range(3):
        sums[a + 1] = d_invariant * vector[a] * (2.0 * message_scale * vector_scale)

    pltpu.make_async_remote_copy(
        src_ref=planes_out.at[pl.ds(0, PLANES - 1)],
        dst_ref=planes_in.at[pl.ds(0, PLANES - 1)],
        send_sem=planes_send,
        recv_sem=planes_recv,
        device_id=(gx, gy, gz),
        device_id_type=MESH,
    ).wait_recv()
    plane = [planes_in[:, 0, :], planes_in[:, 1, :]]
    spread = []
    for x, half, at in WINDOWS:
        line = jnp.zeros((NX, 128), F32)
        for j in range(NY):
            piece = plane[half][NX * j : NX * (j + 1)]
            piece = pltpu.roll(piece, (32 * j - at) % 128, 1)
            inside = jnp.logical_and(lane >= 32 * j, lane < 32 * j + HALO_Y)
            line = jnp.where(inside, piece, line)
        spread.append(line)
    spread.append(jnp.zeros((256 - NX * HALO_X, 128), F32))
    lines = jnp.concatenate(spread, axis=0)
    spectrum = dot(along_x_ref[...], dot(lines, along_yt_ref[...], HIGHEST), HIGHEST)
    mode = gz * PLANES + me
    number = jnp.where(mode <= CZ * NZ // 2, mode, mode - CZ * NZ // 2).astype(F32)
    wave = number * (2.0 * math.pi / (CZ * NZ))
    square = square_ref[...] + wave * wave
    positive = square > 0.0
    safe = jnp.where(positive, square, 1.0)
    filtered = spectrum * jnp.where(
        positive, 4.0 * math.pi * jnp.exp(-square / (4.0 * ewald_beta_sq)) / safe, 0.0
    )
    lines = dot(dot(along_xt_ref[...], filtered, HIGHEST), along_y_ref[...], HIGHEST)
    for j in range(NY):
        for half in range(2):
            piece = jnp.zeros((NX, 128), F32)
            for x, which, at in WINDOWS:
                if which == half:
                    line = pltpu.roll(lines[NX * x : NX * (x + 1)], (at - 32 * j) % 128, 1)
                    inside = jnp.logical_and(lane >= at, lane < at + HALO_Y)
                    piece = jnp.where(inside, line, piece)
            back_out[NX * j : NX * (j + 1), half, :] = piece

    def back_copy(x, y, p):
        return pltpu.make_async_remote_copy(
            src_ref=back_out.at[p],
            dst_ref=back_in.at[me],
            send_sem=back_send,
            recv_sem=back_recv,
            device_id=(x, y, gz),
            device_id_type=MESH,
        )

    over_planes(lambda x, y, p: back_copy(x, y, p).start())
    back_in[me] = back_out[me]

    pushed[...] = jnp.zeros_like(pushed)

    def derive(pair, total):
        k = 2 * pair
        pushes = []
        for e in range(2):
            rel = relatives[k + e]
            along = [jnp.broadcast_to(rel[a : a + 1], (8, ATOMS)) for a in range(3)]
            stretch = jnp.zeros((8, ATOMS), F32)
            direct = [jnp.zeros((8, ATOMS), F32) for _ in range(3)]
            for c in range(0, CHANNELS, 8):
                at = pl.ds(c, 8)
                message = messages[k + e, at, :]
                d_message = sums[0, at, :]
                for a in range(3):
                    d_vector = sums[a + 1, at, :]
                    d_message += d_vector * along[a]
                    direct[a] += d_vector * message
                stretch += d_message * turned[k + e, at, :]
            pull = jnp.sum(stretch, axis=0, keepdims=True) * inverses[k + e][0:1]
            rows = [jnp.sum(direct[a], axis=0, keepdims=True) + pull * rel[a : a + 1] for a in range(3)]
            push = jnp.concatenate(rows + [jnp.zeros((5, ATOMS), F32)], axis=0)
            total = total + push
            pushes.append(push)
        push = jnp.concatenate(pushes, axis=1)
        high = jnp.concatenate([highs[pl.ds(k, 1), :], highs[pl.ds(k + 1, 1), :]], axis=1)
        push_high, push_low = halves(push)
        masks = [high == h for h in range(BLOCKS)]
        left = jnp.concatenate(
            [jnp.where(mask, push_high, 0.0) for mask in masks]
            + [jnp.where(mask, push_low, 0.0) for mask in masks],
            axis=0,
        ).astype(BF16)
        pushed[...] += dot_nt(left, hots[pair])
        return total

    pulled = lax.fori_loop(0, NEIGHBORS // 2, derive, jnp.zeros((8, ATOMS), F32))
    reach = pushed[0 : 8 * BLOCKS, :] + pushed[8 * BLOCKS : 16 * BLOCKS, :]
    for s, a, b, c in LENT:
        h, q = s // 4 + 1, s % 4
        piece = reach[8 * h : 8 * (h + 1), 128 * (q // 2) : 128 * (q // 2 + 1)]
        grads_out[s] = pltpu.roll(piece, 64, 1) if q % 2 else piece

    def grads_copy(s, a, b, c):
        return pltpu.make_async_remote_copy(
            src_ref=grads_out.at[s],
            dst_ref=grads_in.at[s],
            send_sem=grads_send.at[s],
            recv_sem=grads_recv.at[s],
            device_id=shifted(a, b, c),
            device_id_type=MESH,
        )

    for slot in LENT:
        grads_copy(*slot).start()

    pltpu.make_async_remote_copy(
        src_ref=back_out.at[pl.ds(0, PLANES - 1)],
        dst_ref=back_in.at[pl.ds(0, PLANES - 1)],
        send_sem=back_send,
        recv_sem=back_recv,
        device_id=(gx, gy, gz),
        device_id_type=MESH,
    ).wait_recv()
    modes[gz, :, 0:128] = back_in[:, 0, :]
    modes[gz, :, 128:256] = back_in[:, 1, :]

    def mode_copy(c):
        return pltpu.make_async_remote_copy(
            src_ref=modes.at[gz],
            dst_ref=modes.at[gz],
            send_sem=modes_send.at[c],
            recv_sem=modes_recv.at[NZ - c],
            device_id=(gx, gy, lax.rem(gz + c, NZ)),
            device_id_type=MESH,
        )

    def mode_arrival(c):
        l = lax.rem(gz + c, NZ)
        return pltpu.make_async_remote_copy(
            src_ref=modes.at[gz],
            dst_ref=modes.at[l],
            send_sem=modes_send.at[c],
            recv_sem=modes_recv.at[c],
            device_id=(gx, gy, l),
            device_id_type=MESH,
        )

    for c in range(1, NZ):
        mode_copy(c).start()

    for slot in LENT:
        grads_copy(*slot).wait_recv()
    returned = grads_in[LENT[0][0]]
    for slot in LENT[1:]:
        returned = returned + grads_in[slot[0]]
    keep = jnp.where(lax.broadcasted_iota(jnp.int32, (128, ATOMS), 0) < EXPORTED, pick, 0.0)
    grad = reach[0:8] - pulled + dot(returned, keep, HIGHEST)

    for c in range(1, NZ):
        mode_arrival(c).wait_recv()
    field = dot(
        jnp.concatenate([modes[l] for l in range(NZ)], axis=0), window[...], HIGHEST
    )
    here_waves = z_waves[...]
    potential = jnp.sum(here_waves * field[:, 0:ATOMS], axis=0, keepdims=True)
    along_first = jnp.sum(here_waves * field[:, ATOMS : 2 * ATOMS], axis=0, keepdims=True)
    along_second = jnp.sum(here_waves * field[:, 2 * ATOMS :], axis=0, keepdims=True)
    along_third = jnp.sum(z_slopes[...] * field[:, 0:ATOMS], axis=0, keepdims=True)
    forces_ref[0:1, :] = -(grad[0:1] + charge * along_first)
    forces_ref[1:2, :] = -(grad[1:2] + charge * along_second)
    forces_ref[2:3, :] = -(grad[2:3] + charge * along_third)
    atom_energy_ref[...] = short + 0.5 * charge * potential

    for c in range(1, NZ):
        part_copy(c).wait_send()
        mode_copy(c).wait_send()
    for slot in LENT:
        lend_copy(*slot).wait_send()
        grads_copy(*slot).wait_send()
    pltpu.make_async_remote_copy(
        src_ref=planes_out.at[pl.ds(0, PLANES - 1)],
        dst_ref=planes_in.at[pl.ds(0, PLANES - 1)],
        send_sem=planes_send,
        recv_sem=planes_recv,
        device_id=(gx, gy, gz),
        device_id_type=MESH,
    ).wait_send()
    pltpu.make_async_remote_copy(
        src_ref=back_out.at[pl.ds(0, PLANES - 1)],
        dst_ref=back_in.at[pl.ds(0, PLANES - 1)],
        send_sem=back_send,
        recv_sem=back_recv,
        device_id=(gx, gy, gz),
        device_id_type=MESH,
    ).wait_send()


def per_device(
    atom_cell,
    atom_frac,
    features,
    ghost_export,
    neighbors,
    neighbor_count,
    w_up,
    radial_weight,
    w_out,
    energy_weight,
    charge_weight,
):
    vmem = pl.BlockSpec(memory_space=pltpu.VMEM)
    constants = tables()
    dma = pltpu.SemaphoreType.DMA
    forces, atom_energy = pl.pallas_call(
        kernel,
        name="layer",
        out_shape=(
            jax.ShapeDtypeStruct((3, ATOMS), F32),
            jax.ShapeDtypeStruct((1, ATOMS), F32),
        ),
        in_specs=[vmem] * (11 + len(constants)),
        out_specs=(vmem, vmem),
        scratch_shapes=[
            pltpu.VMEM((NZ, PLANES, 256), F32),
            pltpu.VMEM((NZ, PLANES, 256), F32),
            pltpu.VMEM((PLANES, 2, 128), F32),
            pltpu.VMEM((PLANES, 2, 128), F32),
            pltpu.VMEM((PLANES, 2, 128), F32),
            pltpu.VMEM((PLANES, 2, 128), F32),
            pltpu.VMEM((NZ, PLANES, 256), F32),
            pltpu.VMEM((EXPORTED + 16, 128), BF16),
            pltpu.VMEM((28, EXPORTED + 16, 128), BF16),
            pltpu.VMEM((27, 8, 128), F32),
            pltpu.VMEM((27, 8, 128), F32),
            pltpu.VMEM((16, ATOMS), F32),
            pltpu.VMEM((CZ * NZ, ATOMS), F32),
            pltpu.VMEM((CZ * NZ, ATOMS), F32),
            pltpu.VMEM((256, 3 * ATOMS), F32),
            pltpu.VMEM((BLOCKS * ROWS, 256), BF16),
            pltpu.VMEM((BLOCKS * ROWS, 2 * ATOMS), F32),
            pltpu.VMEM((2 * CHANNELS, 2 * ATOMS), F32),
            pltpu.VMEM((NEIGHBORS, CHANNELS, ATOMS), F32),
            pltpu.VMEM((NEIGHBORS, CHANNELS, ATOMS), F32),
            pltpu.VMEM((NEIGHBORS // 2, 256, 2 * ATOMS), BF16),
            pltpu.VMEM((NEIGHBORS, ATOMS), jnp.int32),
            pltpu.VMEM((NEIGHBORS, ATOMS), jnp.int32),
            pltpu.VMEM((NEIGHBORS, 8, ATOMS), F32),
            pltpu.VMEM((NEIGHBORS, 8, ATOMS), F32),
            pltpu.VMEM((4, CHANNELS, ATOMS), F32),
            pltpu.VMEM((16 * BLOCKS, 256), F32),
            dma((NZ,)),
            dma((NZ,)),
            dma,
            dma,
            dma,
            dma,
            dma((NZ,)),
            dma((NZ,)),
            dma((27,)),
            dma((27,)),
            dma((27,)),
            dma((27,)),
        ],
        compiler_params=pltpu.CompilerParams(collective_id=0, has_side_effects=True),
    )(
        atom_cell,
        atom_frac,
        features,
        jnp.concatenate([ghost_export, ghost_export]).reshape(1, 2 * EXPORTED),
        neighbors,
        neighbor_count.reshape(1, ATOMS),
        w_up,
        radial_weight,
        w_out,
        energy_weight.reshape(1, CHANNELS),
        charge_weight.reshape(1, CHANNELS),
        *constants,
    )
    return forces, atom_energy.reshape(ATOMS)


def solution(mesh):
    whole = ("gx", "gy", "gz")
    in_specs = (
        P(None, whole),
        P(None, whole),
        P(None, whole),
        P(whole),
        P(whole, None),
        P(whole),
        P(),
        P(),
        P(),
        P(),
        P(),
    )
    out_specs = (P(None, whole), P(whole))
    return jax.shard_map(
        per_device, mesh=mesh, in_specs=in_specs, out_specs=out_specs, check_vma=False
    )
```

profile of v0, /device:TPU:2, one launch (start us, length us, event | category | flops | bytes accessed | tf_op | source)
XLA Modules:
  0.0 64.8 jit_solution(10216479721146116025)
XLA Ops:
  0.6 0.0 copy-start.1
  0.6 0.0 copy-start.4
  0.6 0.7 %copy-done.4 = s32[64]{0:T(128)S(1)} copy-done((s32[64]{0:T(128)S(1)}, s32[64]{0:T(128)}, u32[]{:S(2)}) %copy-start.4) | copy-done | bytes 280
  1.3 0.6 add_bitcast_fusion.export_ref
  1.9 0.0 copy-done.1
  1.9 0.0 copy-start
  1.9 0.7 %copy.20.radial_ref = f32[128,8]{1,0:T(8,128)} copy(f32[128,8]{0,1:T(8,128)S(1)} %copy-done.1) | data formatting | bytes 8192 | tf_op args[7]
  2.6 0.0 copy-done
  2.6 0.7 %copy.19.neighbor_ref = s32[256,32]{1,0:T(8,128)} copy(s32[256,32]{0,1:T(8,128)S(1)} %copy-done) | data formatting | bytes 65536 | tf_op args[4]
  3.4 59.5 %layer.1 = (f32[3,256]{1,0:T(4,128)}, f32[1,256]{1,0:T(1,128)}) custom-call(s32[3,256]{1,0:T(4,128)} %cell_ref.1, bf16[3,256]{1,0:T(4,128)(2,1)} %frac_ref.1, bf16[128,256]{1,0:T(8,128)(2,1)} %feat_ref.1, s32[1,128]{1,0:T(1,128)} %add_bitcast_fusion.export_ref, s32[256,32]{1,0:T(8,128)} %copy.19.neighbor_ref, s32[1,256]{1,0:T(1,128)} %bitcast.6, ...), custom_call_target="tpu_custom_call" | custom-call | tf_op jit(solution)/shard_map/layer/pallas_call | solution.py:634
  62.9 0.0 copy-start.2
  62.9 0.7 %copy-done.2 = f32[3,256]{1,0:T(4,128)S(1)} copy-done((f32[3,256]{1,0:T(4,128)S(1)}, f32[3,256]{1,0:T(4,128)}, u32[]{:S(2)}) %copy-start.2) | copy-done | bytes 3096
  63.6 0.0 copy-start.3
  63.6 0.6 copy.23
  64.2 0.1 copy-done.3
  64.3 0.6 copy.24
Async XLA Ops:
  0.6 1.3 %copy-start.1 = (f32[128,8]{0,1:T(8,128)S(1)}, f32[128,8]{0,1:T(8,128)}, u32[]{:S(2)}) copy-start(f32[128,8]{0,1:T(8,128)} %param.24) | copy-start | bytes 12292
  0.6 0.7 %copy-start.4 = (s32[64]{0:T(128)S(1)}, s32[64]{0:T(128)}, u32[]{:S(2)}) copy-start(s32[64]{0:T(128)} %param.20) | copy-start | bytes 772
  1.9 0.8 %copy-start = (s32[256,32]{0,1:T(8,128)S(1)}, s32[256,32]{0,1:T(8,128)}, u32[]{:S(2)}) copy-start(s32[256,32]{0,1:T(8,128)} %param.21) | copy-start | bytes 98308
  62.9 0.7 %copy-start.2 = (f32[3,256]{1,0:T(4,128)S(1)}, f32[3,256]{1,0:T(4,128)}, u32[]{:S(2)}) copy-start(f32[3,256]{1,0:T(4,128)} %get-tuple-element.8) | copy-start | bytes 9220
  63.6 0.7 %copy-start.3 = (f32[1,256]{1,0:T(1,128)S(1)}, f32[1,256]{1,0:T(1,128)}, u32[]{:S(2)}) copy-start(f32[1,256]{1,0:T(1,128)} %get-tuple-element.5) | copy-start | bytes 3076
where the time goes:
time: 65.1 us; the launch traced here: 64.8 us
  Pallas kernels  59.5 us (91%)
  local copies, waits for them, and re-layouts  4.07 us (6%)
  between operations  0.67 us (1%)
    pallas_call x1, Pallas kernels, per_device(): pl.pallas_call(kernel, name='layer', out_shape=(jax.ShapeDtypeStruct((3,...  59.5 us
    unnamed x14, local copies, waits for them, and re-layouts  4.07 us

commit v1 on v0

--- a/solution.py
+++ b/solution.py
@@ -33,6 +33,7 @@
 
 SLOTS = [(s, s // 9 - 1, s // 3 % 3 - 1, s % 3 - 1) for s in range(27)]
 LENT = [slot for slot in SLOTS if slot[0] != 13]
+BESIDE = [(b, c) for _, a, b, c in LENT if a == 0]
 WINDOWS = [(x, x // PER_HALF, HALO_Y * (x % PER_HALF)) for x in range(HALO_X)]
 
 
@@ -137,7 +138,6 @@
     back_out,
     back_in,
     modes,
-    lend_out,
     ghosts,
     grads_out,
     grads_in,
@@ -147,6 +147,7 @@
     window,
     table,
     gathered,
+    partial,
     radials,
     messages,
     turned,
@@ -165,13 +166,21 @@
     back_recv,
     modes_send,
     modes_recv,
-    lend_send,
-    lend_recv,
+    beside_send,
+    beside_recv,
+    far_send,
+    far_recv,
+    beyond_send,
+    beyond_recv,
+    near_send,
+    near_recv,
     grads_send,
     grads_recv,
 ):
     gx, gy, gz = lax.axis_index("gx"), lax.axis_index("gy"), lax.axis_index("gz")
     me = gy * NX + gx
+    odd = lax.rem(gx, 2)
+    near, far = 1 - 2 * odd, 2 * odd - 1
 
     def shifted(a, b, c):
         return (lax.rem(gx + a + NX, NX), lax.rem(gy + b + NY, NY), lax.rem(gz + c + NZ, NZ))
@@ -206,11 +215,11 @@
     place[0:3, :] = cell.astype(F32)
     place[8:11, :] = frac
     spot = place[...]
-    export = export_ref[...]
+    export = jnp.concatenate([export_ref[...], export_ref[...]], axis=1)
     pick_t = (lax.broadcasted_iota(jnp.int32, (ATOMS, 128), 0) == export).astype(F32)
     pick = pick_t.T
-    lend_out[0:EXPORTED, :] = dot_nt(pick[0:EXPORTED].astype(BF16), up).astype(BF16)
-    lend_out[EXPORTED : EXPORTED + 16, :] = dot(spot.astype(BF16), pick_t.astype(BF16)).astype(BF16)
+    ghosts[13, 0:EXPORTED, :] = dot_nt(pick[0:EXPORTED].astype(BF16), up).astype(BF16)
+    ghosts[13, EXPORTED : EXPORTED + 16, :] = dot(spot.astype(BF16), pick_t.astype(BF16)).astype(BF16)
 
     values, slopes = spline_weights(frac)
     along_z = along_z_ref[gz]
@@ -227,6 +236,32 @@
     for l in range(NZ):
         parts_out[l] = waves[PLANES * l : PLANES * (l + 1)]
 
+    z_slopes[...] = dot(
+        along_z, node_rows(128, cell[2:3], [v[2:3] for v in slopes]), HIGHEST
+    )
+    slope_x = node_rows(16, cell[0:1], [v[0:1] for v in slopes])
+    slope_y = node_rows(24, cell[1:2], [v[1:2] for v in slopes])
+    for x, half, lane in WINDOWS:
+        at = pl.ds(128 * half + lane, HALO_Y)
+        window[at, ATOMS : 2 * ATOMS] = slope_x[x : x + 1] * rows_y[0:HALO_Y]
+        window[at, 2 * ATOMS : 3 * ATOMS] = rows_x[x : x + 1] * slope_y[0:HALO_Y]
+    entry = neighbor_ref[...]
+    lows[...] = entry & 255
+    highs[...] = entry >> 8
+    sub = lax.broadcasted_iota(jnp.int32, (ATOMS, 2 * ATOMS), 0)
+
+    def two_rows(ref, k):
+        return jnp.concatenate([ref[pl.ds(k, 1), :], ref[pl.ds(k + 1, 1), :]], axis=1)
+
+    def heat(pair, carry):
+        hots[pair] = jnp.where(sub == two_rows(lows, 2 * pair), 1.0, 0.0).astype(BF16)
+        return carry
+
+    lax.fori_loop(0, NEIGHBORS // 2, heat, 0)
+    ghosts[27] = jnp.zeros((EXPORTED + 16, 128), BF16)
+    table[0, 0:CHANNELS, :] = up
+    table[0, CHANNELS:ROWS, :] = spot.astype(BF16)
+
     pl.semaphore_wait(barrier, (NZ - 1) + (PLANES - 1) + len(LENT))
 
     def part_copy(c):
@@ -251,35 +286,55 @@
             device_id_type=MESH,
         )
 
-    def lend_copy(s, a, b, c):
+    def remote(source, target, send, recv, device):
         return pltpu.make_async_remote_copy(
-            src_ref=lend_out,
-            dst_ref=ghosts.at[s],
-            send_sem=lend_send.at[s],
-            recv_sem=lend_recv.at[s],
-            device_id=shifted(-a, -b, -c),
+            src_ref=source,
+            dst_ref=target,
+            send_sem=send,
+            recv_sem=recv,
+            device_id=device,
             device_id_type=MESH,
         )
 
+    def far_copy(side):
+        return remote(
+            ghosts.at[13], ghosts.at[9 * (side + 1) + 4], far_send, far_recv, shifted(far, 0, 0)
+        )
+
+    def beside_copy(n):
+        b, c = BESIDE[n]
+        slot = 9 + 3 * (b + 1) + (c + 1)
+        return remote(
+            ghosts.at[13], ghosts.at[slot], beside_send.at[n], beside_recv.at[n], shifted(0, -b, -c)
+        )
+
+    def beyond_copy(n):
+        b, c = BESIDE[n]
+        slot = 9 * (far + 1) + 3 * (b + 1) + (c + 1)
+        return remote(
+            ghosts.at[9 * (far + 1) + 4],
+            ghosts.at[slot],
+            beyond_send.at[n],
+            beyond_recv.at[n],
+            shifted(0, -b, -c),
+        )
+
+    def near_copy(side):
+        return remote(
+            ghosts.at[pl.ds(9, 9)],
+            ghosts.at[pl.ds(9 * (side + 1), 9)],
+            near_send,
+            near_recv,
+            shifted(near, 0, 0),
+        )
+
+    far_copy(-far).start()
     for c in range(1, NZ):
         part_copy(c).start()
-    for slot in LENT:
-        lend_copy(*slot).start()
-
-    z_slopes[...] = dot(
-        along_z, node_rows(128, cell[2:3], [v[2:3] for v in slopes]), HIGHEST
-    )
-    slope_x = node_rows(16, cell[0:1], [v[0:1] for v in slopes])
-    slope_y = node_rows(24, cell[1:2], [v[1:2] for v in slopes])
-    for x, half, lane in WINDOWS:
-        at = pl.ds(128 * half + lane, HALO_Y)
-        window[at, ATOMS : 2 * ATOMS] = slope_x[x : x + 1] * rows_y[0:HALO_Y]
-        window[at, 2 * ATOMS : 3 * ATOMS] = rows_x[x : x + 1] * slope_y[0:HALO_Y]
+    for n in range(8):
+        beside_copy(n).start()
+
     parts_in[gz] = parts_out[gz]
-    ghosts[13] = jnp.zeros((EXPORTED + 16, 128), BF16)
-    ghosts[27] = jnp.zeros((EXPORTED + 16, 128), BF16)
-    table[0:CHANNELS, :] = up
-    table[CHANNELS:ROWS, :] = spot.astype(BF16)
 
     for c in range(1, NZ):
         part_arrival(c).wait_recv()
@@ -300,128 +355,62 @@
     over_planes(lambda x, y, p: plane_copy(x, y, p).start())
     planes_in[me] = planes_out[me]
 
-    for slot in LENT:
-        lend_copy(*slot).wait_recv()
+    for n in range(8):
+        beside_copy(n).wait_recv()
+    near_copy(-near).start()
+    far_copy(far).wait_recv()
+    for n in range(8):
+        beyond_copy(n).start()
     row = lax.broadcasted_iota(jnp.int32, (16, 128), 0)
     lane = lax.broadcasted_iota(jnp.int32, (16, 128), 1)
-    for h in range(1, BLOCKS):
+
+    def enter(h):
         first = 4 * (h - 1)
         lent = jnp.concatenate([ghosts[first + q, 0:EXPORTED, :] for q in range(4)], axis=0)
-        table[ROWS * h : ROWS * h + CHANNELS, :] = lent.astype(F32).T.astype(BF16)
+        table[h, 0:CHANNELS, :] = lent.astype(F32).T.astype(BF16)
         spots = []
         for q in range(4):
             s = first + q
-            a, b, c = (s // 9 - 1, s // 3 % 3 - 1, s % 3 - 1)
-            far = jnp.where(
-                row == 0,
-                float(a * CX),
-                jnp.where(row == 1, float(b * CY), jnp.where(row == 2, float(c * CZ), 0.0)),
+            a, b, c = s // 9 - 1, lax.rem(s // 3, 3) - 1, lax.rem(s, 3) - 1
+            away = jnp.where(
+                row == 0, a * CX, jnp.where(row == 1, b * CY, jnp.where(row == 2, c * CZ, 0))
             )
-            spots.append(ghosts[s, EXPORTED : EXPORTED + 16, :].astype(F32) + far)
-        at = slice(ROWS * h + CHANNELS, ROWS * (h + 1))
-        table[at, 0:128] = jnp.where(lane < EXPORTED, spots[0], spots[1]).astype(BF16)
-        table[at, 128:256] = jnp.where(lane < EXPORTED, spots[2], spots[3]).astype(BF16)
-
-    entry = neighbor_ref[...]
-    eye = (
-        lax.broadcasted_iota(jnp.int32, (NEIGHBORS, NEIGHBORS), 0)
-        == lax.broadcasted_iota(jnp.int32, (NEIGHBORS, NEIGHBORS), 1)
-    ).astype(BF16)
-    lows[...] = dot_nt(eye, (entry & 255).astype(F32).astype(BF16)).astype(jnp.int32)
-    highs[...] = dot_nt(eye, (entry >> 8).astype(F32).astype(BF16)).astype(jnp.int32)
+            spots.append(
+                ghosts[s, EXPORTED : EXPORTED + 16, :].astype(F32) + away.astype(F32)
+            )
+        table[h, CHANNELS:ROWS, 0:128] = jnp.where(lane < EXPORTED, spots[0], spots[1]).astype(BF16)
+        table[h, CHANNELS:ROWS, 128:256] = jnp.where(lane < EXPORTED, spots[2], spots[3]).astype(BF16)
+
+    near_copy(near).wait_recv()
+    soon, late = 4 - 3 * odd, 1 + 4 * odd
+
+    def enter_soon(n, carry):
+        enter(soon + n)
+        return carry
+
+    lax.fori_loop(0, 4, enter_soon, 0)
+
+    def gather_soon(pair, carry):
+        hot = hots[pair]
+        gathered[0:ROWS, :] = dot(table[0], hot)
+        gathered[ROWS : 5 * ROWS, :] = dot(
+            table[pl.ds(soon, 4)].reshape(4 * ROWS, 256), hot
+        )
+        high8 = jnp.broadcast_to(two_rows(highs, 2 * pair), (8, 2 * ATOMS)) - soon
+        for r in range(0, ROWS, 8):
+            at = pl.ds(r, 8)
+            result = gathered[at, :]
+            for n in range(4):
+                result = jnp.where(high8 == n, gathered[pl.ds(ROWS * (n + 1) + r, 8), :], result)
+            partial[pair, at, :] = result
+        return carry
+
+    lax.fori_loop(0, NEIGHBORS // 2, gather_soon, 0)
 
     weight_high, weight_low = halves(radial_ref[...])
-    stack = lax.broadcasted_iota(jnp.int32, (8, 24), 1)
-    basis_row = lax.broadcasted_iota(jnp.int32, (8, 24), 0)
-    hit = lax.rem(stack, 8) == basis_row
-    to_high = jnp.logical_and(hit, stack < 16).astype(BF16)
-    to_low = jnp.logical_and(hit, stack >= 16).astype(BF16)
-    weights = (
-        dot(weight_high.astype(BF16), to_high) + dot(weight_low.astype(BF16), to_low)
-    ).astype(BF16)
-
-    here = spot[0:8] + spot[8:16]
-    count = count_ref[...]
-    for a in range(4):
-        sums[a] = jnp.zeros((CHANNELS, ATOMS), F32)
-    sub = lax.broadcasted_iota(jnp.int32, (ATOMS, 2 * ATOMS), 0)
-    centre = lax.broadcasted_iota(jnp.int32, (8, 2 * ATOMS), 0).astype(F32) * basis_step
-
-    def gather(pair, carry):
-        k = 2 * pair
-        low = jnp.concatenate([lows[pl.ds(k, 1), :], lows[pl.ds(k + 1, 1), :]], axis=1)
-        high = jnp.concatenate([highs[pl.ds(k, 1), :], highs[pl.ds(k + 1, 1), :]], axis=1)
-        hot = jnp.where(sub == low, 1.0, 0.0).astype(BF16)
-        hots[pair] = hot
-        gathered[...] = dot(table[...], hot)
-        high8 = jnp.broadcast_to(high, (8, 2 * ATOMS))
-
-        def chosen(start):
-            result = gathered[pl.ds(start, 8), :]
-            for h in range(1, BLOCKS):
-                result = jnp.where(high8 == h, gathered[pl.ds(start + ROWS * h, 8), :], result)
-            return result
-
-        there = chosen(CHANNELS) + chosen(CHANNELS + 8)
-        rel = there - jnp.concatenate([here, here], axis=1)
-        dist = jnp.sqrt(jnp.sum(rel * rel, axis=0, keepdims=True) + 1.0)
-        used = jnp.concatenate([count > k, count > k + 1], axis=1).astype(F32)
-        gap = (dist - centre) / basis_width
-        basis = jnp.exp(-(gap * gap)) * used
-        slope = basis * gap * (-2.0 / basis_width)
-        basis_high, basis_low = halves(basis)
-        slope_high, slope_low = halves(slope)
-        radials[0:CHANNELS, :] = dot(
-            weights, jnp.concatenate([basis_high, basis_low, basis_high], axis=0).astype(BF16)
-        )
-        radials[CHANNELS : 2 * CHANNELS, :] = dot(
-            weights, jnp.concatenate([slope_high, slope_low, slope_high], axis=0).astype(BF16)
-        )
-        inverse = 1.0 / dist
-        relatives[k] = rel[:, 0:ATOMS]
-        relatives[k + 1] = rel[:, ATOMS:]
-        inverses[k] = jnp.broadcast_to(inverse[:, 0:ATOMS], (8, ATOMS))
-        inverses[k + 1] = jnp.broadcast_to(inverse[:, ATOMS:], (8, ATOMS))
-        along = [jnp.broadcast_to(rel[a : a + 1], (8, 2 * ATOMS)) for a in range(3)]
-        for c in range(0, CHANNELS, 8):
-            at = pl.ds(c, 8)
-            source = chosen(c)
-            message = radials[at, :] * source
-            turn = radials[pl.ds(CHANNELS + c, 8), :] * source
-            messages[k, at, :] = message[:, 0:ATOMS]
-            messages[k + 1, at, :] = message[:, ATOMS:]
-            turned[k, at, :] = turn[:, 0:ATOMS]
-            turned[k + 1, at, :] = turn[:, ATOMS:]
-            sums[0, at, :] += message[:, 0:ATOMS] + message[:, ATOMS:]
-            for a in range(3):
-                moved = message * along[a]
-                sums[a + 1, at, :] += moved[:, 0:ATOMS] + moved[:, ATOMS:]
-        return carry
-
-    lax.fori_loop(0, NEIGHBORS // 2, gather, 0)
-
-    scalar = sums[0] * message_scale
-    vector = [sums[a + 1] * (message_scale * vector_scale) for a in range(3)]
-    invariant = scalar + scalar * scalar + (
-        vector[0] * vector[0] + vector[1] * vector[1] + vector[2] * vector[2]
-    )
-    w_out = w_out_ref[...]
-    hidden = feat.astype(F32) + dot(w_out, invariant.astype(BF16))
-    wide = (
-        lax.broadcasted_iota(jnp.int32, (CHANNELS, CHANNELS), 0)
-        == lax.broadcasted_iota(jnp.int32, (CHANNELS, CHANNELS), 1)
-    ).astype(BF16)
-    readout = dot_nt(wide, jnp.broadcast_to(energy_ref[...], (16, CHANNELS)))[:, 0:1]
-    gate = 1.0 / (1.0 + jnp.exp(-hidden))
-    short = jnp.sum(readout * (hidden * gate), axis=0, keepdims=True)
-    d_hidden = readout * (gate * (1.0 + hidden * (1.0 - gate)))
-    back_high, back_low = halves(d_hidden)
-    w_out_t = w_out.astype(F32).T.astype(BF16)
-    d_invariant = dot(w_out_t, back_high.astype(BF16)) + dot(w_out_t, back_low.astype(BF16))
-    d_invariant = d_invariant.astype(BF16).astype(F32)
-    sums[0] = d_invariant * (1.0 + 2.0 * scalar) * message_scale
-    for a in range(3):
-        sums[a + 1] = d_invariant * vector[a] * (2.0 * message_scale * vector_scale)
+    weights = jnp.concatenate(
+        [weight_high, weight_high, weight_low, jnp.zeros((104, CHANNELS), F32)], axis=0
+    ).T[:, 0:24].astype(BF16)
 
     pltpu.make_async_remote_copy(
         src_ref=planes_out.at[pl.ds(0, PLANES - 1)],
@@ -477,6 +466,127 @@
     over_planes(lambda x, y, p: back_copy(x, y, p).start())
     back_in[me] = back_out[me]
 
+    for n in range(8):
+        beyond_copy(n).wait_recv()
+
+    def enter_late(n, carry):
+        enter(late + n)
+        return carry
+
+    lax.fori_loop(0, 3, enter_late, 0)
+    here = spot[0:8] + spot[8:16]
+    count = count_ref[...]
+    for a in range(4):
+        sums[a] = jnp.zeros((CHANNELS, ATOMS), F32)
+    centre = lax.broadcasted_iota(jnp.int32, (8, 2 * ATOMS), 0).astype(F32) * basis_step
+
+    def gather(pair, carry):
+        k = 2 * pair
+        gathered[0 : 3 * ROWS, :] = dot(table[pl.ds(late, 3)].reshape(3 * ROWS, 256), hots[pair])
+        high8 = jnp.broadcast_to(two_rows(highs, k), (8, 2 * ATOMS)) - late
+
+        def chosen(start):
+            result = partial[pair, pl.ds(start, 8), :]
+            for n in range(3):
+                result = jnp.where(high8 == n, gathered[pl.ds(start + ROWS * n, 8), :], result)
+            return result
+
+        there = chosen(CHANNELS) + chosen(CHANNELS + 8)
+        rel = there - jnp.concatenate([here, here], axis=1)
+        dist = jnp.sqrt(jnp.sum(rel * rel, axis=0, keepdims=True) + 1.0)
+        used = jnp.concatenate([count > k, count > k + 1], axis=1).astype(F32)
+        gap = (dist - centre) / basis_width
+        basis = jnp.exp(-(gap * gap)) * used
+        slope = basis * gap * (-2.0 / basis_width)
+        basis_high, basis_low = halves(basis)
+        slope_high, slope_low = halves(slope)
+        radials[0:CHANNELS, :] = dot(
+            weights, jnp.concatenate([basis_high, basis_low, basis_high], axis=0).astype(BF16)
+        )
+        radials[CHANNELS : 2 * CHANNELS, :] = dot(
+            weights, jnp.concatenate([slope_high, slope_low, slope_high], axis=0).astype(BF16)
+        )
+        inverse = 1.0 / dist
+        relatives[k] = rel[:, 0:ATOMS]
+        relatives[k + 1] = rel[:, ATOMS:]
+        inverses[k] = jnp.broadcast_to(inverse[:, 0:ATOMS], (8, ATOMS))
+        inverses[k + 1] = jnp.broadcast_to(inverse[:, ATOMS:], (8, ATOMS))
+        along = [jnp.broadcast_to(rel[a : a + 1], (8, 2 * ATOMS)) for a in range(3)]
+        for c in range(0, CHANNELS, 8):
+            at = pl.ds(c, 8)
+            source = chosen(c)
+            message = radials[at, :] * source
+            turn = radials[pl.ds(CHANNELS + c, 8), :] * source
+            messages[k, at, :] = message[:, 0:ATOMS]
+            messages[k + 1, at, :] = message[:, ATOMS:]
+            turned[k, at, :] = turn[:, 0:ATOMS]
+            turned[k + 1, at, :] = turn[:, ATOMS:]
+            sums[0, at, :] += message[:, 0:ATOMS] + message[:, ATOMS:]
+            for a in range(3):
+                moved = message * along[a]
+                sums[a + 1, at, :] += moved[:, 0:ATOMS] + moved[:, ATOMS:]
+        return carry
+
+    lax.fori_loop(0, NEIGHBORS // 2, gather, 0)
+
+    scalar = sums[0] * message_scale
+    vector = [sums[a + 1] * (message_scale * vector_scale) for a in range(3)]
+    invariant = scalar + scalar * scalar + (
+        vector[0] * vector[0] + vector[1] * vector[1] + vector[2] * vector[2]
+    )
+    w_out = w_out_ref[...]
+    hidden = feat.astype(F32) + dot(w_out, invariant.astype(BF16))
+    wide = (
+        lax.broadcasted_iota(jnp.int32, (CHANNELS, CHANNELS), 0)
+        == lax.broadcasted_iota(jnp.int32, (CHANNELS, CHANNELS), 1)
+    ).astype(BF16)
+    readout = dot_nt(wide, jnp.broadcast_to(energy_ref[...], (16, CHANNELS)))[:, 0:1]
+    gate = 1.0 / (1.0 + jnp.exp(-hidden))
+    short = jnp.sum(readout * (hidden * gate), axis=0, keepdims=True)
+    d_hidden = readout * (gate * (1.0 + hidden * (1.0 - gate)))
+    back_high, back_low = halves(d_hidden)
+    w_out_t = w_out.astype(F32).T.astype(BF16)
+    d_invariant = dot(w_out_t, back_high.astype(BF16)) + dot(w_out_t, back_low.astype(BF16))
+    d_invariant = d_invariant.astype(BF16).astype(F32)
+    sums[0] = d_invariant * (1.0 + 2.0 * scalar) * message_scale
+    for a in range(3):
+        sums[a + 1] = d_invariant * vector[a] * (2.0 * message_scale * vector_scale)
+
+    pltpu.make_async_remote_copy(
+        src_ref=back_out.at[pl.ds(0, PLANES - 1)],
+        dst_ref=back_in.at[pl.ds(0, PLANES - 1)],
+        send_sem=back_send,
+        recv_sem=back_recv,
+        device_id=(gx, gy, gz),
+        device_id_type=MESH,
+    ).wait_recv()
+    modes[gz, :, 0:128] = back_in[:, 0, :]
+    modes[gz, :, 128:256] = back_in[:, 1, :]
+
+    def mode_copy(c):
+        return pltpu.make_async_remote_copy(
+            src_ref=modes.at[gz],
+            dst_ref=modes.at[gz],
+            send_sem=modes_send.at[c],
+            recv_sem=modes_recv.at[NZ - c],
+            device_id=(gx, gy, lax.rem(gz + c, NZ)),
+            device_id_type=MESH,
+        )
+
+    def mode_arrival(c):
+        l = lax.rem(gz + c, NZ)
+        return pltpu.make_async_remote_copy(
+            src_ref=modes.at[gz],
+            dst_ref=modes.at[l],
+            send_sem=modes_send.at[c],
+            recv_sem=modes_recv.at[c],
+            device_id=(gx, gy, l),
+            device_id_type=MESH,
+        )
+
+    for c in range(1, NZ):
+        mode_copy(c).start()
+
     pushed[...] = jnp.zeros_like(pushed)
 
     def derive(pair, total):
@@ -502,7 +612,7 @@
             total = total + push
             pushes.append(push)
         push = jnp.concatenate(pushes, axis=1)
-        high = jnp.concatenate([highs[pl.ds(k, 1), :], highs[pl.ds(k + 1, 1), :]], axis=1)
+        high = two_rows(highs, k)
         push_high, push_low = halves(push)
         masks = [high == h for h in range(BLOCKS)]
         left = jnp.concatenate(
@@ -518,7 +628,7 @@
     for s, a, b, c in LENT:
         h, q = s // 4 + 1, s % 4
         piece = reach[8 * h : 8 * (h + 1), 128 * (q // 2) : 128 * (q // 2 + 1)]
-        grads_out[s] = pltpu.roll(piece, 64, 1) if q % 2 else piece
+        grads_out[s] = (pltpu.roll(piece, 64, 1) if q % 2 else piece)[0:4]
 
     def grads_copy(s, a, b, c):
         return pltpu.make_async_remote_copy(
@@ -533,47 +643,13 @@
     for slot in LENT:
         grads_copy(*slot).start()
 
-    pltpu.make_async_remote_copy(
-        src_ref=back_out.at[pl.ds(0, PLANES - 1)],
-        dst_ref=back_in.at[pl.ds(0, PLANES - 1)],
-        send_sem=back_send,
-        recv_sem=back_recv,
-        device_id=(gx, gy, gz),
-        device_id_type=MESH,
-    ).wait_recv()
-    modes[gz, :, 0:128] = back_in[:, 0, :]
-    modes[gz, :, 128:256] = back_in[:, 1, :]
-
-    def mode_copy(c):
-        return pltpu.make_async_remote_copy(
-            src_ref=modes.at[gz],
-            dst_ref=modes.at[gz],
-            send_sem=modes_send.at[c],
-            recv_sem=modes_recv.at[NZ - c],
-            device_id=(gx, gy, lax.rem(gz + c, NZ)),
-            device_id_type=MESH,
-        )
-
-    def mode_arrival(c):
-        l = lax.rem(gz + c, NZ)
-        return pltpu.make_async_remote_copy(
-            src_ref=modes.at[gz],
-            dst_ref=modes.at[l],
-            send_sem=modes_send.at[c],
-            recv_sem=modes_recv.at[c],
-            device_id=(gx, gy, l),
-            device_id_type=MESH,
-        )
-
-    for c in range(1, NZ):
-        mode_copy(c).start()
-
     for slot in LENT:
         grads_copy(*slot).wait_recv()
     returned = grads_in[LENT[0][0]]
     for slot in LENT[1:]:
         returned = returned + grads_in[slot[0]]
     keep = jnp.where(lax.broadcasted_iota(jnp.int32, (128, ATOMS), 0) < EXPORTED, pick, 0.0)
+    returned = jnp.concatenate([returned, jnp.zeros((4, 128), F32)], axis=0)
     grad = reach[0:8] - pulled + dot(returned, keep, HIGHEST)
 
     for c in range(1, NZ):
@@ -594,8 +670,12 @@
     for c in range(1, NZ):
         part_copy(c).wait_send()
         mode_copy(c).wait_send()
+    far_copy(-far).wait_send()
+    near_copy(-near).wait_send()
+    for n in range(8):
+        beside_copy(n).wait_send()
+        beyond_copy(n).wait_send()
     for slot in LENT:
-        lend_copy(*slot).wait_send()
         grads_copy(*slot).wait_send()
     pltpu.make_async_remote_copy(
         src_ref=planes_out.at[pl.ds(0, PLANES - 1)],
@@ -648,16 +728,16 @@
             pltpu.VMEM((PLANES, 2, 128), F32),
             pltpu.VMEM((PLANES, 2, 128), F32),
             pltpu.VMEM((NZ, PLANES, 256), F32),
-            pltpu.VMEM((EXPORTED + 16, 128), BF16),
             pltpu.VMEM((28, EXPORTED + 16, 128), BF16),
-            pltpu.VMEM((27, 8, 128), F32),
-            pltpu.VMEM((27, 8, 128), F32),
+            pltpu.VMEM((27, 4, 128), F32),
+            pltpu.VMEM((27, 4, 128), F32),
             pltpu.VMEM((16, ATOMS), F32),
             pltpu.VMEM((CZ * NZ, ATOMS), F32),
             pltpu.VMEM((CZ * NZ, ATOMS), F32),
             pltpu.VMEM((256, 3 * ATOMS), F32),
-            pltpu.VMEM((BLOCKS * ROWS, 256), BF16),
-            pltpu.VMEM((BLOCKS * ROWS, 2 * ATOMS), F32),
+            pltpu.VMEM((BLOCKS, ROWS, 256), BF16),
+            pltpu.VMEM((5 * ROWS, 2 * ATOMS), F32),
+            pltpu.VMEM((NEIGHBORS // 2, ROWS, 2 * ATOMS), F32),
             pltpu.VMEM((2 * CHANNELS, 2 * ATOMS), F32),
             pltpu.VMEM((NEIGHBORS, CHANNELS, ATOMS), F32),
             pltpu.VMEM((NEIGHBORS, CHANNELS, ATOMS), F32),
@@ -676,8 +756,14 @@
             dma,
             dma((NZ,)),
             dma((NZ,)),
-            dma((27,)),
-            dma((27,)),
+            dma((8,)),
+            dma((8,)),
+            dma,
+            dma,
+            dma((8,)),
+            dma((8,)),
+            dma,
+            dma,
             dma((27,)),
             dma((27,)),
         ],
@@ -686,11 +772,11 @@
         atom_cell,
         atom_frac,
         features,
-        jnp.concatenate([ghost_export, ghost_export]).reshape(1, 2 * EXPORTED),
-        neighbors,
+        ghost_export.reshape(1, EXPORTED),
+        neighbors.T,
         neighbor_count.reshape(1, ATOMS),
         w_up,
-        radial_weight,
+        radial_weight.T,
         w_out,
         energy_weight.reshape(1, CHANNELS),
         charge_weight.reshape(1, CHANNELS),

time: 65.1 us -> 56 us (0.86)
  Pallas kernels: 59.5 us -> 53.1 us
  local copies, waits for them, and re-layouts: 4.07 us -> 1.87 us
    pallas_call x1, Pallas kernels: 59.5 us -> 53.1 us  [per_device(): pl.pallas_call(kernel, name='layer', out_shape=(jax.ShapeDtypeStruct((3,...]
    unnamed x14 -> x6, local copies, waits for them, and re-layouts: 4.07 us -> 1.87 us
where the time goes in v1:
time: 56 us; the launch traced here: 55.6 us
  Pallas kernels  53.1 us (95%)
  local copies, waits for them, and re-layouts  1.87 us (3%)
  between operations  0.65 us (1%)
    pallas_call x1, Pallas kernels, per_device(): pl.pallas_call(kernel, name='layer', out_shape=(jax.ShapeDtypeStruct((3,...  53.1 us
    unnamed x6, local copies, waits for them, and re-layouts  1.87 us

profile of v1, /device:TPU:2, one launch (start us, length us, event | category | flops | bytes accessed | tf_op | source)
XLA Modules:
  0.0 55.6 jit_solution(6610270068286032617)
XLA Ops:
  0.6 53.1 %layer.1 = (f32[3,256]{1,0:T(4,128)}, f32[1,256]{1,0:T(1,128)}) custom-call(s32[3,256]{1,0:T(4,128)} %cell_ref.1, bf16[3,256]{1,0:T(4,128)(2,1)} %frac_ref.1, bf16[128,256]{1,0:T(8,128)(2,1)} %feat_ref.1, s32[1,64]{1,0:T(1,128)} %bitcast.11, s32[32,256]{1,0:T(8,128)} %bitcast.7, s32[1,256]{1,0:T(1,128)} %bitcast.10, bf16[128,128]{1,0:T(8,128)(2,1)} %w_up_ref.1, ...), custom_call_target="tpu_custom_call" | custom-call | tf_op jit(solution)/shard_map/layer/pallas_call | solution.py:714
  53.7 0.0 copy-start
  53.7 0.7 %copy-done = f32[3,256]{1,0:T(4,128)S(1)} copy-done((f32[3,256]{1,0:T(4,128)S(1)}, f32[3,256]{1,0:T(4,128)}, u32[]{:S(2)}) %copy-start) | copy-done | bytes 3096
  54.4 0.0 copy-start.1
  54.4 0.6 %copy.21 = f32[3,256]{1,0:T(4,128)} copy(f32[3,256]{1,0:T(4,128)S(1)} %copy-done) | data formatting | bytes 6144
  55.0 0.0 copy-done.1
  55.0 0.6 %copy.22 = f32[256]{0:T(256)} copy(f32[256]{0:T(256)S(1)} %bitcast.9) | data formatting | bytes 2048
Async XLA Ops:
  53.7 0.7 %copy-start = (f32[3,256]{1,0:T(4,128)S(1)}, f32[3,256]{1,0:T(4,128)}, u32[]{:S(2)}) copy-start(f32[3,256]{1,0:T(4,128)} %get-tuple-element.8) | copy-start | bytes 9220
  54.4 0.6 %copy-start.1 = (f32[1,256]{1,0:T(1,128)S(1)}, f32[1,256]{1,0:T(1,128)}, u32[]{:S(2)}) copy-start(f32[1,256]{1,0:T(1,128)} %get-tuple-element.5) | copy-start | bytes 3076

commit v2 on v1

--- a/solution.py
+++ b/solution.py
@@ -155,7 +155,6 @@
     lows,
     highs,
     relatives,
-    inverses,
     sums,
     pushed,
     parts_send,
@@ -253,14 +252,17 @@
     def two_rows(ref, k):
         return jnp.concatenate([ref[pl.ds(k, 1), :], ref[pl.ds(k + 1, 1), :]], axis=1)
 
-    def heat(pair, carry):
-        hots[pair] = jnp.where(sub == two_rows(lows, 2 * pair), 1.0, 0.0).astype(BF16)
-        return carry
-
-    lax.fori_loop(0, NEIGHBORS // 2, heat, 0)
     ghosts[27] = jnp.zeros((EXPORTED + 16, 128), BF16)
     table[0, 0:CHANNELS, :] = up
     table[0, CHANNELS:ROWS, :] = spot.astype(BF16)
+
+    def gather_own(pair, carry):
+        hot = jnp.where(sub == two_rows(lows, 2 * pair), 1.0, 0.0).astype(BF16)
+        hots[pair] = hot
+        partial[pair] = dot(table[0, 0:ROWS, :], hot).astype(BF16)
+        return carry
+
+    lax.fori_loop(0, NEIGHBORS // 2, gather_own, 0)
 
     pl.semaphore_wait(barrier, (NZ - 1) + (PLANES - 1) + len(LENT))
 
@@ -390,18 +392,20 @@
 
     lax.fori_loop(0, 4, enter_soon, 0)
 
+    def blocks_of(k, first):
+        block = (two_rows(highs, k) - first).astype(F32)
+        return jnp.broadcast_to(block, (16, 2 * ATOMS)).astype(BF16)
+
     def gather_soon(pair, carry):
-        hot = hots[pair]
-        gathered[0:ROWS, :] = dot(table[0], hot)
-        gathered[ROWS : 5 * ROWS, :] = dot(
-            table[pl.ds(soon, 4)].reshape(4 * ROWS, 256), hot
-        )
-        high8 = jnp.broadcast_to(two_rows(highs, 2 * pair), (8, 2 * ATOMS)) - soon
-        for r in range(0, ROWS, 8):
-            at = pl.ds(r, 8)
-            result = gathered[at, :]
+        gathered[...] = dot(
+            table[pl.ds(soon, 4), 0:ROWS, :].reshape(4 * ROWS, 256), hots[pair]
+        ).astype(BF16)
+        block = blocks_of(2 * pair, soon)
+        for r in range(0, ROWS, 16):
+            at = pl.ds(r, 16)
+            result = partial[pair, at, :]
             for n in range(4):
-                result = jnp.where(high8 == n, gathered[pl.ds(ROWS * (n + 1) + r, 8), :], result)
+                result = jnp.where(block == n, gathered[pl.ds(ROWS * n + r, 16), :], result)
             partial[pair, at, :] = result
         return carry
 
@@ -411,6 +415,74 @@
     weights = jnp.concatenate(
         [weight_high, weight_high, weight_low, jnp.zeros((104, CHANNELS), F32)], axis=0
     ).T[:, 0:24].astype(BF16)
+
+    for n in range(8):
+        beyond_copy(n).wait_recv()
+
+    def enter_late(n, carry):
+        enter(late + n)
+        return carry
+
+    lax.fori_loop(0, 3, enter_late, 0)
+    here = spot[0:8] + spot[8:16]
+    count = count_ref[...]
+    for a in range(4):
+        sums[a] = jnp.zeros((CHANNELS, ATOMS), F32)
+    centre = lax.broadcasted_iota(jnp.int32, (8, 2 * ATOMS), 0).astype(F32) * basis_step
+
+    def gather(pair, carry):
+        k = 2 * pair
+        gathered[0 : 3 * ROWS, :] = dot(
+            table[pl.ds(late, 3), 0:ROWS, :].reshape(3 * ROWS, 256), hots[pair]
+        ).astype(BF16)
+        block = blocks_of(k, late)
+
+        def chosen(start):
+            result = partial[pair, pl.ds(start, 16), :]
+            for n in range(3):
+                result = jnp.where(block == n, gathered[pl.ds(start + ROWS * n, 16), :], result)
+            return result.astype(F32)
+
+        there = chosen(CHANNELS)
+        there = there[0:8] + there[8:16]
+        rel = there - jnp.concatenate([here, here], axis=1)
+        dist = jnp.sqrt(jnp.sum(rel * rel, axis=0, keepdims=True) + 1.0)
+        used = jnp.concatenate([count > k, count > k + 1], axis=1).astype(F32)
+        gap = (dist - centre) / basis_width
+        basis = jnp.exp(-(gap * gap)) * used
+        slope = basis * gap * (-2.0 / basis_width)
+        basis_high, basis_low = halves(basis)
+        slope_high, slope_low = halves(slope)
+        radials[0:CHANNELS, :] = dot(
+            weights, jnp.concatenate([basis_high, basis_low, basis_high], axis=0).astype(BF16)
+        )
+        radials[CHANNELS : 2 * CHANNELS, :] = dot(
+            weights, jnp.concatenate([slope_high, slope_low, slope_high], axis=0).astype(BF16)
+        )
+        inverse = 1.0 / dist
+        relatives[k, 0:8, :] = rel[:, 0:ATOMS]
+        relatives[k + 1, 0:8, :] = rel[:, ATOMS:]
+        relatives[k, 8:16, :] = jnp.broadcast_to(inverse[:, 0:ATOMS], (8, ATOMS))
+        relatives[k + 1, 8:16, :] = jnp.broadcast_to(inverse[:, ATOMS:], (8, ATOMS))
+        along = [jnp.broadcast_to(rel[a : a + 1], (8, 2 * ATOMS)) for a in range(3)]
+        for c in range(0, CHANNELS, 16):
+            sources = chosen(c)
+            for half in range(2):
+                at = pl.ds(c + 8 * half, 8)
+                source = sources[8 * half : 8 * (half + 1)]
+                message = radials[at, :] * source
+                turn = radials[pl.ds(CHANNELS + c + 8 * half, 8), :] * source
+                messages[k, at, :] = message[:, 0:ATOMS]
+                messages[k + 1, at, :] = message[:, ATOMS:]
+                turned[k, at, :] = turn[:, 0:ATOMS]
+                turned[k + 1, at, :] = turn[:, ATOMS:]
+                sums[0, at, :] += message[:, 0:ATOMS] + message[:, ATOMS:]
+                for a in range(3):
+                    moved = message * along[a]
+                    sums[a + 1, at, :] += moved[:, 0:ATOMS] + moved[:, ATOMS:]
+        return carry
+
+    lax.fori_loop(0, NEIGHBORS // 4, gather, 0)
 
     pltpu.make_async_remote_copy(
         src_ref=planes_out.at[pl.ds(0, PLANES - 1)],
@@ -466,68 +538,7 @@
     over_planes(lambda x, y, p: back_copy(x, y, p).start())
     back_in[me] = back_out[me]
 
-    for n in range(8):
-        beyond_copy(n).wait_recv()
-
-    def enter_late(n, carry):
-        enter(late + n)
-        return carry
-
-    lax.fori_loop(0, 3, enter_late, 0)
-    here = spot[0:8] + spot[8:16]
-    count = count_ref[...]
-    for a in range(4):
-        sums[a] = jnp.zeros((CHANNELS, ATOMS), F32)
-    centre = lax.broadcasted_iota(jnp.int32, (8, 2 * ATOMS), 0).astype(F32) * basis_step
-
-    def gather(pair, carry):
-        k = 2 * pair
-        gathered[0 : 3 * ROWS, :] = dot(table[pl.ds(late, 3)].reshape(3 * ROWS, 256), hots[pair])
-        high8 = jnp.broadcast_to(two_rows(highs, k), (8, 2 * ATOMS)) - late
-
-        def chosen(start):
-            result = partial[pair, pl.ds(start, 8), :]
-            for n in range(3):
-                result = jnp.where(high8 == n, gathered[pl.ds(start + ROWS * n, 8), :], result)
-            return result
-
-        there = chosen(CHANNELS) + chosen(CHANNELS + 8)
-        rel = there - jnp.concatenate([here, here], axis=1)
-        dist = jnp.sqrt(jnp.sum(rel * rel, axis=0, keepdims=True) + 1.0)
-        used = jnp.concatenate([count > k, count > k + 1], axis=1).astype(F32)
-        gap = (dist - centre) / basis_width
-        basis = jnp.exp(-(gap * gap)) * used
-        slope = basis * gap * (-2.0 / basis_width)
-        basis_high, basis_low = halves(basis)
-        slope_high, slope_low = halves(slope)
-        radials[0:CHANNELS, :] = dot(
-            weights, jnp.concatenate([basis_high, basis_low, basis_high], axis=0).astype(BF16)
-        )
-        radials[CHANNELS : 2 * CHANNELS, :] = dot(
-            weights, jnp.concatenate([slope_high, slope_low, slope_high], axis=0).astype(BF16)
-        )
-        inverse = 1.0 / dist
-        relatives[k] = rel[:, 0:ATOMS]
-        relatives[k + 1] = rel[:, ATOMS:]
-        inverses[k] = jnp.broadcast_to(inverse[:, 0:ATOMS], (8, ATOMS))
-        inverses[k + 1] = jnp.broadcast_to(inverse[:, ATOMS:], (8, ATOMS))
-        along = [jnp.broadcast_to(rel[a : a + 1], (8, 2 * ATOMS)) for a in range(3)]
-        for c in range(0, CHANNELS, 8):
-            at = pl.ds(c, 8)
-            source = chosen(c)
-            message = radials[at, :] * source
-            turn = radials[pl.ds(CHANNELS + c, 8), :] * source
-            messages[k, at, :] = message[:, 0:ATOMS]
-            messages[k + 1, at, :] = message[:, ATOMS:]
-            turned[k, at, :] = turn[:, 0:ATOMS]
-            turned[k + 1, at, :] = turn[:, ATOMS:]
-            sums[0, at, :] += message[:, 0:ATOMS] + message[:, ATOMS:]
-            for a in range(3):
-                moved = message * along[a]
-                sums[a + 1, at, :] += moved[:, 0:ATOMS] + moved[:, ATOMS:]
-        return carry
-
-    lax.fori_loop(0, NEIGHBORS // 2, gather, 0)
+    lax.fori_loop(NEIGHBORS // 4, NEIGHBORS // 2, gather, 0)
 
     scalar = sums[0] * message_scale
     vector = [sums[a + 1] * (message_scale * vector_scale) for a in range(3)]
@@ -552,62 +563,32 @@
     for a in range(3):
         sums[a + 1] = d_invariant * vector[a] * (2.0 * message_scale * vector_scale)
 
-    pltpu.make_async_remote_copy(
-        src_ref=back_out.at[pl.ds(0, PLANES - 1)],
-        dst_ref=back_in.at[pl.ds(0, PLANES - 1)],
-        send_sem=back_send,
-        recv_sem=back_recv,
-        device_id=(gx, gy, gz),
-        device_id_type=MESH,
-    ).wait_recv()
-    modes[gz, :, 0:128] = back_in[:, 0, :]
-    modes[gz, :, 128:256] = back_in[:, 1, :]
-
-    def mode_copy(c):
-        return pltpu.make_async_remote_copy(
-            src_ref=modes.at[gz],
-            dst_ref=modes.at[gz],
-            send_sem=modes_send.at[c],
-            recv_sem=modes_recv.at[NZ - c],
-            device_id=(gx, gy, lax.rem(gz + c, NZ)),
-            device_id_type=MESH,
-        )
-
-    def mode_arrival(c):
-        l = lax.rem(gz + c, NZ)
-        return pltpu.make_async_remote_copy(
-            src_ref=modes.at[gz],
-            dst_ref=modes.at[l],
-            send_sem=modes_send.at[c],
-            recv_sem=modes_recv.at[c],
-            device_id=(gx, gy, l),
-            device_id_type=MESH,
-        )
-
-    for c in range(1, NZ):
-        mode_copy(c).start()
-
     pushed[...] = jnp.zeros_like(pushed)
 
     def derive(pair, total):
         k = 2 * pair
+        rel = [relatives[k + e, 0:8, :] for e in range(2)]
+        along = [[jnp.broadcast_to(rel[e][a : a + 1], (8, ATOMS)) for a in range(3)] for e in range(2)]
+        stretch = [jnp.zeros((8, ATOMS), F32) for _ in range(2)]
+        direct = [[jnp.zeros((8, ATOMS), F32) for _ in range(3)] for _ in range(2)]
+        for c in range(0, CHANNELS, 8):
+            at = pl.ds(c, 8)
+            d_scalar = sums[0, at, :]
+            d_vector = [sums[a + 1, at, :] for a in range(3)]
+            for e in range(2):
+                message = messages[k + e, at, :]
+                d_message = d_scalar
+                for a in range(3):
+                    d_message += d_vector[a] * along[e][a]
+                    direct[e][a] += d_vector[a] * message
+                stretch[e] += d_message * turned[k + e, at, :]
         pushes = []
         for e in range(2):
-            rel = relatives[k + e]
-            along = [jnp.broadcast_to(rel[a : a + 1], (8, ATOMS)) for a in range(3)]
-            stretch = jnp.zeros((8, ATOMS), F32)
-            direct = [jnp.zeros((8, ATOMS), F32) for _ in range(3)]
-            for c in range(0, CHANNELS, 8):
-                at = pl.ds(c, 8)
-                message = messages[k + e, at, :]
-                d_message = sums[0, at, :]
-                for a in range(3):
-                    d_vector = sums[a + 1, at, :]
-                    d_message += d_vector * along[a]
-                    direct[a] += d_vector * message
-                stretch += d_message * turned[k + e, at, :]
-            pull = jnp.sum(stretch, axis=0, keepdims=True) * inverses[k + e][0:1]
-            rows = [jnp.sum(direct[a], axis=0, keepdims=True) + pull * rel[a : a + 1] for a in range(3)]
+            pull = jnp.sum(stretch[e], axis=0, keepdims=True) * relatives[k + e, 8:9, :]
+            rows = [
+                jnp.sum(direct[e][a], axis=0, keepdims=True) + pull * rel[e][a : a + 1]
+                for a in range(3)
+            ]
             push = jnp.concatenate(rows + [jnp.zeros((5, ATOMS), F32)], axis=0)
             total = total + push
             pushes.append(push)
@@ -623,7 +604,44 @@
         pushed[...] += dot_nt(left, hots[pair])
         return total
 
-    pulled = lax.fori_loop(0, NEIGHBORS // 2, derive, jnp.zeros((8, ATOMS), F32))
+    pulled = lax.fori_loop(0, NEIGHBORS // 8, derive, jnp.zeros((8, ATOMS), F32))
+
+    pltpu.make_async_remote_copy(
+        src_ref=back_out.at[pl.ds(0, PLANES - 1)],
+        dst_ref=back_in.at[pl.ds(0, PLANES - 1)],
+        send_sem=back_send,
+        recv_sem=back_recv,
+        device_id=(gx, gy, gz),
+        device_id_type=MESH,
+    ).wait_recv()
+    modes[gz, :, 0:128] = back_in[:, 0, :]
+    modes[gz, :, 128:256] = back_in[:, 1, :]
+
+    def mode_copy(c):
+        return pltpu.make_async_remote_copy(
+            src_ref=modes.at[gz],
+            dst_ref=modes.at[gz],
+            send_sem=modes_send.at[c],
+            recv_sem=modes_recv.at[NZ - c],
+            device_id=(gx, gy, lax.rem(gz + c, NZ)),
+            device_id_type=MESH,
+        )
+
+    def mode_arrival(c):
+        l = lax.rem(gz + c, NZ)
+        return pltpu.make_async_remote_copy(
+            src_ref=modes.at[gz],
+            dst_ref=modes.at[l],
+            send_sem=modes_send.at[c],
+            recv_sem=modes_recv.at[c],
+            device_id=(gx, gy, l),
+            device_id_type=MESH,
+        )
+
+    for c in range(1, NZ):
+        mode_copy(c).start()
+
+    pulled = lax.fori_loop(NEIGHBORS // 8, NEIGHBORS // 2, derive, pulled)
     reach = pushed[0 : 8 * BLOCKS, :] + pushed[8 * BLOCKS : 16 * BLOCKS, :]
     for s, a, b, c in LENT:
         h, q = s // 4 + 1, s % 4
@@ -643,6 +661,17 @@
     for slot in LENT:
         grads_copy(*slot).start()
 
+    for c in range(1, NZ):
+        mode_arrival(c).wait_recv()
+    field = dot(
+        jnp.concatenate([modes[l] for l in range(NZ)], axis=0), window[...], HIGHEST
+    )
+    here_waves = z_waves[...]
+    potential = jnp.sum(here_waves * field[:, 0:ATOMS], axis=0, keepdims=True)
+    along_first = jnp.sum(here_waves * field[:, ATOMS : 2 * ATOMS], axis=0, keepdims=True)
+    along_second = jnp.sum(here_waves * field[:, 2 * ATOMS :], axis=0, keepdims=True)
+    along_third = jnp.sum(z_slopes[...] * field[:, 0:ATOMS], axis=0, keepdims=True)
+    atom_energy_ref[...] = short + 0.5 * charge * potential
     for slot in LENT:
         grads_copy(*slot).wait_recv()
     returned = grads_in[LENT[0][0]]
@@ -652,20 +681,9 @@
     returned = jnp.concatenate([returned, jnp.zeros((4, 128), F32)], axis=0)
     grad = reach[0:8] - pulled + dot(returned, keep, HIGHEST)
 
-    for c in range(1, NZ):
-        mode_arrival(c).wait_recv()
-    field = dot(
-        jnp.concatenate([modes[l] for l in range(NZ)], axis=0), window[...], HIGHEST
-    )
-    here_waves = z_waves[...]
-    potential = jnp.sum(here_waves * field[:, 0:ATOMS], axis=0, keepdims=True)
-    along_first = jnp.sum(here_waves * field[:, ATOMS : 2 * ATOMS], axis=0, keepdims=True)
-    along_second = jnp.sum(here_waves * field[:, 2 * ATOMS :], axis=0, keepdims=True)
-    along_third = jnp.sum(z_slopes[...] * field[:, 0:ATOMS], axis=0, keepdims=True)
     forces_ref[0:1, :] = -(grad[0:1] + charge * along_first)
     forces_ref[1:2, :] = -(grad[1:2] + charge * along_second)
     forces_ref[2:3, :] = -(grad[2:3] + charge * along_third)
-    atom_energy_ref[...] = short + 0.5 * charge * potential
 
     for c in range(1, NZ):
         part_copy(c).wait_send()
@@ -715,8 +733,8 @@
         kernel,
         name="layer",
         out_shape=(
-            jax.ShapeDtypeStruct((3, ATOMS), F32),
-            jax.ShapeDtypeStruct((1, ATOMS), F32),
+            pltpu.VMEM((3, ATOMS), F32),
+            pltpu.VMEM((1, ATOMS), F32),
         ),
         in_specs=[vmem] * (11 + len(constants)),
         out_specs=(vmem, vmem),
@@ -729,23 +747,22 @@
             pltpu.VMEM((PLANES, 2, 128), F32),
             pltpu.VMEM((NZ, PLANES, 256), F32),
             pltpu.VMEM((28, EXPORTED + 16, 128), BF16),
-            pltpu.VMEM((27, 4, 128), F32),
-            pltpu.VMEM((27, 4, 128), F32),
+            pltpu.VMEM((32, 4, 128), F32),
+            pltpu.VMEM((32, 4, 128), F32),
             pltpu.VMEM((16, ATOMS), F32),
             pltpu.VMEM((CZ * NZ, ATOMS), F32),
             pltpu.VMEM((CZ * NZ, ATOMS), F32),
             pltpu.VMEM((256, 3 * ATOMS), F32),
-            pltpu.VMEM((BLOCKS, ROWS, 256), BF16),
-            pltpu.VMEM((5 * ROWS, 2 * ATOMS), F32),
-            pltpu.VMEM((NEIGHBORS // 2, ROWS, 2 * ATOMS), F32),
+            pltpu.VMEM((BLOCKS, CHANNELS + 32, 256), BF16),
+            pltpu.VMEM((4 * ROWS, 2 * ATOMS), BF16),
+            pltpu.VMEM((NEIGHBORS // 2, ROWS, 2 * ATOMS), BF16),
             pltpu.VMEM((2 * CHANNELS, 2 * ATOMS), F32),
             pltpu.VMEM((NEIGHBORS, CHANNELS, ATOMS), F32),
             pltpu.VMEM((NEIGHBORS, CHANNELS, ATOMS), F32),
             pltpu.VMEM((NEIGHBORS // 2, 256, 2 * ATOMS), BF16),
             pltpu.VMEM((NEIGHBORS, ATOMS), jnp.int32),
             pltpu.VMEM((NEIGHBORS, ATOMS), jnp.int32),
-            pltpu.VMEM((NEIGHBORS, 8, ATOMS), F32),
-            pltpu.VMEM((NEIGHBORS, 8, ATOMS), F32),
+            pltpu.VMEM((NEIGHBORS, 16, ATOMS), F32),
             pltpu.VMEM((4, CHANNELS, ATOMS), F32),
             pltpu.VMEM((16 * BLOCKS, 256), F32),
             dma((NZ,)),

time: 56 us -> 54.3 us (0.970)
  local copies, waits for them, and re-layouts: 1.87 us -> 1.16 us
  Pallas kernels: 53.1 us -> 52.4 us
    unnamed x6 -> x2, local copies, waits for them, and re-layouts: 1.87 us -> 1.16 us
    pallas_call x1, Pallas kernels: 53.1 us -> 52.4 us  [per_device(): pl.pallas_call(kernel, name='layer', out_shape=(pltpu.VMEM((3, ATOMS), F3...]
where the time goes in v2:
time: 54.3 us; the launch traced here: 54.2 us
  Pallas kernels  52.4 us (97%)
  local copies, waits for them, and re-layouts  1.16 us (2%)
  between operations  0.64 us (1%)
    pallas_call x1, Pallas kernels, per_device(): pl.pallas_call(kernel, name='layer', out_shape=(pltpu.VMEM((3, ATOMS), F3...  52.4 us
    unnamed x2, local copies, waits for them, and re-layouts  1.16 us

profile of v2, /device:TPU:2, one launch (start us, length us, event | category | flops | bytes accessed | tf_op | source)
XLA Modules:
  0.0 54.2 jit_solution(5741614499655349748)
XLA Ops:
  0.6 52.4 %layer.1 = (f32[3,256]{1,0:T(4,128)S(1)}, f32[1,256]{1,0:T(1,128)S(1)}) custom-call(s32[3,256]{1,0:T(4,128)} %cell_ref.1, bf16[3,256]{1,0:T(4,128)(2,1)} %frac_ref.1, bf16[128,256]{1,0:T(8,128)(2,1)} %feat_ref.1, s32[1,64]{1,0:T(1,128)} %bitcast.11, s32[32,256]{1,0:T(8,128)} %bitcast.8, s32[1,256]{1,0:T(1,128)} %bitcast.10, bf16[128,128]{1,0:T(8,128)(2,1)} %w_up_ref.1, ...), custom_call_target="tpu_custom_call" | custom-call | tf_op jit(solution)/shard_map/layer/pallas_call | solution.py:732
  53.1 0.6 %copy.21 = f32[3,256]{1,0:T(4,128)} copy(f32[3,256]{1,0:T(4,128)S(1)} %get-tuple-element.6) | data formatting | bytes 6144
  53.7 0.6 %copy.22 = f32[256]{0:T(256)} copy(f32[256]{0:T(256)S(1)} %bitcast.7) | data formatting | bytes 2048

commit v3 on v1

--- a/solution.py
+++ b/solution.py
@@ -715,8 +715,8 @@
         kernel,
         name="layer",
         out_shape=(
-            jax.ShapeDtypeStruct((3, ATOMS), F32),
-            jax.ShapeDtypeStruct((1, ATOMS), F32),
+            pltpu.VMEM((3, ATOMS), F32),
+            pltpu.VMEM((1, ATOMS), F32),
         ),
         in_specs=[vmem] * (11 + len(constants)),
         out_specs=(vmem, vmem),

time: 56 us -> 54.7 us (0.977)
  local copies, waits for them, and re-layouts: 1.87 us -> 1.16 us
  Pallas kernels: 53.1 us -> 52.5 us
    unnamed x6 -> x2, local copies, waits for them, and re-layouts: 1.87 us -> 1.16 us
    pallas_call x1, Pallas kernels: 53.1 us -> 52.5 us  [per_device(): pl.pallas_call(kernel, name='layer', out_shape=(pltpu.VMEM((3, ATOMS), F3...]
where the time goes in v3:
time: 54.7 us; the launch traced here: 54.3 us
  Pallas kernels  52.5 us (96%)
  local copies, waits for them, and re-layouts  1.16 us (2%)
  between operations  0.64 us (1%)
    pallas_call x1, Pallas kernels, per_device(): pl.pallas_call(kernel, name='layer', out_shape=(pltpu.VMEM((3, ATOMS), F3...  52.5 us
    unnamed x2, local copies, waits for them, and re-layouts  1.16 us

profile of v3, /device:TPU:2, one launch (start us, length us, event | category | flops | bytes accessed | tf_op | source)
XLA Modules:
  0.0 54.3 jit_solution(13025228615576211596)
XLA Ops:
  0.6 52.5 %layer.1 = (f32[3,256]{1,0:T(4,128)S(1)}, f32[1,256]{1,0:T(1,128)S(1)}) custom-call(s32[3,256]{1,0:T(4,128)} %cell_ref.1, bf16[3,256]{1,0:T(4,128)(2,1)} %frac_ref.1, bf16[128,256]{1,0:T(8,128)(2,1)} %feat_ref.1, s32[1,64]{1,0:T(1,128)} %bitcast.11, s32[32,256]{1,0:T(8,128)} %bitcast.8, s32[1,256]{1,0:T(1,128)} %bitcast.10, bf16[128,128]{1,0:T(8,128)(2,1)} %w_up_ref.1, ...), custom_call_target="tpu_custom_call" | custom-call | tf_op jit(solution)/shard_map/layer/pallas_call | solution.py:714
  53.1 0.6 %copy.21 = f32[3,256]{1,0:T(4,128)} copy(f32[3,256]{1,0:T(4,128)S(1)} %get-tuple-element.6) | data formatting | bytes 6144
  53.7 0.6 %copy.22 = f32[256]{0:T(256)} copy(f32[256]{0:T(256)S(1)} %bitcast.7) | data formatting | bytes 2048
